TPU v7x, 128 devices: a whole 4x4x4 slice. The times are simulated.
128 devices in a mesh: grp: 4 (over y), dev: 32 (over z, x, core).
Axes of the slice: x: 4, y: 4, z: 4, core: 2. Of those that a mesh axis runs over, the one named last changes fastest.
Arguments:
- feeder_state: float32 [12288, 24, 256], P(('grp', 'dev')), may hold values from -6 to 6
- feeder_load: bfloat16 [12288, 24, 256], P(('grp', 'dev')), may hold values from -6 to 6
- feeder_inverse: bfloat16 [12288, 256, 256], P(('grp', 'dev')), as said below
- coupling: bfloat16 [12288, 256], P(('grp', 'dev')), may hold values from -0.375 to 0.375
- feeder_bus: int32 [12288], P(('grp', 'dev')), may hold values from 0 to 16383
- bus_coupling: bfloat16 [16384, 16384], P(('grp', 'dev')), may hold values from -0.09375 to 0.09375
- bus_diagonal: float32 [16384], P(('grp', 'dev')), may hold values from 1 to 3
- bus_load: float32 [24, 16384], P(None, ('grp', 'dev')), may hold values from -6 to 6
- bus_state: float32 [24, 16384], P(None, ('grp', 'dev')), may hold values from -6 to 6
- barrier: float32 [2], replicated, may hold values from 0.5 to 4
- step_length: float32 [2], replicated, may hold values from 0.4 to 1
Outputs:
- feeder_final: float32 [12288, 24, 256], P(('grp', 'dev'))
- bus_final: float32 [24, 16384], P(None, ('grp', 'dev'))
Inputs may be any that keep to these rules, and one draw needn't show every extreme that they name: `feeder_inverse`: each block is symmetric with a positive diagonal and is positive definite.
All inputs are finite; a program needn't handle non-finite values.
Results may differ from a plain program's by a relative error of at most 0.0022.
Values may be sent and summed in bfloat16 or wider, within the bound.
A program may use at most 128 MiB of HBM per device.

v0:
```python
import jax
import jax.numpy as jnp
from jax import lax
from jax.sharding import Mesh
from jax.sharding import PartitionSpec as P

GRP_DEV = ("grp", "dev_0", "dev_1", "dev_2")


def turned_gather(arrays, axis, dims):
    turned = [jnp.moveaxis(a, dim, 0) for a, dim in zip(arrays, dims)]
    widths = [t[0].size for t in turned]
    both = jnp.concatenate([t.reshape(-1, w) for t, w in zip(turned, widths)], axis=1)
    filled = lax.all_gather(both, axis, axis=0, tiled=True)
    blocks = jnp.split(filled, [sum(widths[:k]) for k in range(1, len(widths))], axis=1)
    return tuple(
        (
            jnp.moveaxis(b.reshape(-1, *t.shape[1:]), 0, dim)
            for b, t, dim in zip(blocks, turned, dims)
        )
    )


def from_everyone(array, axis):
    copies = jnp.broadcast_to(array, (lax.axis_size(axis), *array.shape))
    return lax.all_to_all(copies, axis, split_axis=0, concat_axis=0, tiled=True)


def joined_along(blocks, dim):
    blocks = jnp.moveaxis(blocks, 0, dim)
    lengths = blocks.shape
    return blocks.reshape(*lengths[:dim], lengths[dim] * lengths[dim + 1], *lengths[dim + 2 :])


def gather_axes(array, axes, dim):
    far, near = axes
    leading = from_everyone(array, far)
    blocks = jnp.swapaxes(from_everyone(leading, near), 0, 1)
    return joined_along(blocks.reshape(-1, *array.shape), dim)


def on_device(
    feeder_state,
    feeder_load,
    feeder_inverse,
    coupling,
    feeder_bus,
    bus_coupling,
    bus_diagonal,
    bus_load,
    bus_state,
    barrier,
    step_length,
):
    highest = lax.Precision.HIGHEST
    sensitivity = coupling.astype(jnp.float32)
    response = jnp.einsum(
        "fij,fj->fi", feeder_inverse, coupling, preferred_element_type=jnp.float32
    )
    schur = jnp.sum(sensitivity * response, axis=-1)
    bus_local = bus_coupling.shape[0]
    schur_all, buses_all = turned_gather((schur, feeder_bus.astype(jnp.float32)), GRP_DEV, (0, 0))
    bus_first = lax.axis_index(GRP_DEV) * bus_local
    owned = (
        buses_all.astype(jnp.int32)[:, None]
        == bus_first + jnp.arange(bus_local, dtype=jnp.int32)[None, :]
    ).astype(jnp.float32)
    bus_schur = jnp.dot(schur_all, owned, precision=highest)
    feeder_now = feeder_state
    bus_now = bus_state
    for iteration in range(barrier.shape[0]):
        weight_mu = barrier[iteration]
        residual = (
            feeder_load.astype(jnp.float32) + weight_mu * jax.nn.sigmoid(-feeder_now)
        ).astype(jnp.bfloat16)
        solved = jnp.einsum(
            "fij,fhj->fhi", feeder_inverse, residual, preferred_element_type=jnp.float32
        )
        boundary = jnp.sum(solved * sensitivity[:, None, :], axis=-1)
        boundary_all = gather_axes(boundary.T, (("grp", "dev_0", "dev_1"), "dev_2"), 1)
        bus_totals = jnp.dot(boundary_all, owned, precision=highest)
        bus_right = bus_load + weight_mu * jax.nn.sigmoid(-bus_now) - bus_totals
        pivots = bus_diagonal + weight_mu + bus_schur
        first_sweep = (bus_right / pivots).astype(jnp.bfloat16)
        coupled = jnp.einsum(
            "hk,bk->hb",
            gather_axes(first_sweep, (("grp", "dev_0", "dev_1"), "dev_2"), 1),
            bus_coupling,
            preferred_element_type=jnp.float32,
        )
        second_sweep = (bus_right - coupled) / pivots
        bus_now = bus_now + step_length[iteration] * second_sweep
        all_steps = gather_axes(second_sweep, (("grp", "dev_0", "dev_1"), "dev_2"), 1)
        at_feeder = jnp.take(all_steps, feeder_bus, axis=1)
        feeder_now = feeder_now + step_length[iteration] * (
            solved - response[:, None, :] * at_feeder.T[:, :, None]
        )
    return (feeder_now, bus_now)


def solution(mesh):
    split = Mesh(
        mesh.devices.reshape(mesh.shape["grp"], 4, 4, 2), ("grp", "dev_0", "dev_1", "dev_2")
    )
    in_specs = (
        P(GRP_DEV, None, None),
        P(GRP_DEV, None, None),
        P(GRP_DEV, None, None),
        P(GRP_DEV, None),
        P(GRP_DEV),
        P(GRP_DEV, None),
        P(GRP_DEV),
        P(None, GRP_DEV),
        P(None, GRP_DEV),
        P(),
        P(),
    )
    out_specs = (P(GRP_DEV, None, None), P(None, GRP_DEV))
    return jax.shard_map(
        on_device, mesh=split, in_specs=in_specs, out_specs=out_specs, check_vma=False
    )
```

profile of v0, /device:TPU:1, one launch (start us, length us, event | category | flops | bytes accessed | tf_op | source)
XLA Modules:
  0.0 255.7 jit_solution(10424992593101645294)
XLA Ops:
  0.6 1.3 fusion.43
  2.0 0.8 convert_element_type.29
  2.8 11.1 %multiply_reduce_fusion.1 = (f32[96,24]{1,0:T(8,128)S(1)}, f32[96,24,256]{2,1,0:T(8,128)}) fusion(f32[96,256]{1,0:T(8,128)S(1)} %convert_element_type.29, bf16[96,256,256]{2,1,0:T(8,128)(2,1)} %param.15, bf16[96,24,256]{2,1,0:T(8,128)(2,1)} %param.14, f32[96,24,256]{2,1,0:T(8,128)} %param.13, f32[]{:T(128)} %bitcast.1), kind=kOutput, calls=%fused_computation.21 | convolution fusion | flops 306706176 | bytes 18588676 | tf_op jit(solution)/shard_map/fij,fhj->fhi/dot_general | solution.py:76
  13.9 1.0 broadcast_in_dim.57
  14.9 12.0 %all-to-all-start = ((f32[64,24,96]{2,1,0:T(8,128)}), f32[64,24,96]{2,1,0:T(8,128)S(1)}, u32[]{:S(2)}, u32[]{:S(2)}) async-start(f32[64,24,96]{2,1,0:T(8,128)} %broadcast_in_dim.57), calls=%async_computation | async-start | bytes 1572864 | tf_op jit(solution)/shard_map/all_to_all | solution.py:26
  26.9 7.9 %fusion.37 = f32[96,1,256]{2,1,0:T(1,128)S(1)} fusion(bf16[96,256,256]{2,1,0:T(8,128)(2,1)} %param.15, bf16[96,256,1]{1,0,2:T(8,128)(2,1)S(1)} %bitcast.86), kind=kOutput, calls=%fused_computation.40 | convolution fusion | flops 12582912 | bytes 12730368 | tf_op jit(solution)/shard_map/fij,fj->fi/dot_general | solution.py:57
  34.8 0.1 multiply_reduce_fusion.2
  35.0 36.9 %all-gather = f32[128,96,2]{1,2,0:T(2,128)S(1)} all-gather(f32[1,96,2]{1,2,0:T(2,128)S(1)} %maximum_bitcast_fusion), channel_id=1, replica_groups=mesh['grp'=4,'dev_0'=4,'dev_1'=4,'dev_2'=2] {'grp','dev_0','dev_1','dev_2'}, dimensions={0}, use_global_device_ids=true | all-gather | bytes 99072 | tf_op jit(solution)/shard_map/all_gather | solution.py:14
  71.9 0.2 reshape.100
  72.2 3.9 %add_add_fusion = (f32[128]{0:T(128)S(1)}, f32[128]{0:T(128)S(1)}) fusion(f32[128]{0:T(128)S(1)} %copy-done.7, f32[]{:T(128)} %bitcast.24, f32[]{:T(128)} %bitcast.1, s32[128]{0:T(128)S(1)} %iota_add_fusion, s32[12288]{0:T(1024)S(1)} %bitcast.89, f32[12288,2]{0,1:T(2,128)S(1)} %reshape.100), kind=kOutput, calls=%fused_computation.55 | convolution fusion | flops 20447744 | bytes 100360 | tf_op jit(solution)/shard_map/dot_general | solution.py:68
  76.1 0.1 broadcast_in_dim.58
  76.2 4.8 %all_to_all.60 = f32[2,64,24,96]{3,2,1,0:T(8,128)S(1)} all-to-all(f32[2,64,24,96]{3,2,1,0:T(8,128)S(1)} %broadcast_in_dim.58), channel_id=1, replica_groups=mesh['grp'=4,'dev_0'=4,'dev_1'=4,'dev_2'=2] {'dev_2'}, dimensions={0} | all-to-all | bytes 2359296 | tf_op jit(solution)/shard_map/all_to_all | solution.py:26
  81.0 0.1 copy.36
  81.2 0.3 copy.37
  81.5 0.9 reshape.67
  82.4 3.3 %divide_convert_fusion.1 = (bf16[24,128]{1,0:T(8,128)(2,1)S(1)}, f32[24,128]{1,0:T(8,128)S(1)}) fusion(f32[128]{0:T(128)S(1)} %get-tuple-element.4, f32[24,12288]{1,0:T(8,128)S(1)} %reshape.67, s32[128]{0:T(128)S(1)} %iota_add_fusion, s32[12288]{0:T(1024)S(1)} %bitcast.90, f32[24,128]{1,0:T(8,128)S(1)} %copy-done.6, f32[24,128]{1,0:T(8,128)S(1)} %copy-done.3, ...), kind=kOutput, calls=%fused_computation.50 | convolution fusion | flops 454579200 | bytes 1272836 | tf_op jit(solution)/shard_map/dot_general | solution.py:81
  85.8 17.1 %all_to_all.61 = bf16[64,24,128]{2,1,0:T(8,128)(2,1)S(1)} all-to-all(bf16[64,24,128]{2,1,0:T(8,128)(2,1)S(1)} %broadcast_in_dim.59), channel_id=1, replica_groups=mesh['grp'=4,'dev_0'=4,'dev_1'=4,'dev_2'=2] {'grp','dev_0','dev_1'}, dimensions={0} | all-to-all | bytes 786432 | tf_op jit(solution)/shard_map/all_to_all | solution.py:26
  102.9 0.1 broadcast_in_dim.60
  103.0 6.1 %all_to_all.62 = bf16[2,64,24,128]{3,2,1,0:T(8,128)(2,1)S(1)} all-to-all(bf16[2,64,24,128]{3,2,1,0:T(8,128)(2,1)S(1)} %broadcast_in_dim.60), channel_id=1, replica_groups=mesh['grp'=4,'dev_0'=4,'dev_1'=4,'dev_2'=2] {'dev_2'}, dimensions={0} | all-to-all | bytes 1572864 | tf_op jit(solution)/shard_map/all_to_all | solution.py:26
  109.2 1.2 fusion.29
  110.4 1.0 broadcast_in_dim.61
  111.4 4.6 %all-to-all-start.4 = ((f32[64,24,128]{2,1,0:T(8,128)}), f32[64,24,128]{2,1,0:T(8,128)S(1)}, u32[]{:S(2)}, u32[]{:S(2)}) async-start(f32[64,24,128]{2,1,0:T(8,128)} %broadcast_in_dim.61), calls=%async_computation.4 | async-start | bytes 1572864 | tf_op jit(solution)/shard_map/all_to_all | solution.py:26
  116.1 0.6 fusion.42
  116.7 14.9 %all-to-all-done.4 = f32[64,24,128]{2,1,0:T(8,128)S(1)} async-done(((f32[64,24,128]{2,1,0:T(8,128)}), f32[64,24,128]{2,1,0:T(8,128)S(1)}, u32[]{:S(2)}, u32[]{:S(2)}) %all-to-all-start.4) | async-done | bytes 786464 | tf_op jit(solution)/shard_map/all_to_all | solution.py:26
  131.6 0.1 broadcast_in_dim.62
  131.7 6.2 %all_to_all.63 = f32[2,64,24,128]{3,2,1,0:T(8,128)S(1)} all-to-all(f32[2,64,24,128]{3,2,1,0:T(8,128)S(1)} %broadcast_in_dim.62), channel_id=1, replica_groups=mesh['grp'=4,'dev_0'=4,'dev_1'=4,'dev_2'=2] {'dev_2'}, dimensions={0} | all-to-all | bytes 3145728 | tf_op jit(solution)/shard_map/all_to_all | solution.py:26
  137.9 0.1 copy.41
  138.0 4.6 %copy.42 = f32[24,128,128]{0,2,1:T(8,128)} copy(f32[24,128,128]{2,0,1:T(8,128)S(1)} %bitcast.80) | data formatting | bytes 3145728 | tf_op jit(solution)/shard_map/transpose | solution.py:30
  142.7 4.0 %gather_fusion = f32[96,24]{1,0:T(8,128)S(1)} fusion(f32[24,16384]{0,1:T(8,128)} %bitcast.77, s32[1024]{0:T(1024)S(1)} %pad_clamp_fusion), kind=kCustom, calls=%fused_computation.clone | custom fusion | bytes 18816 | tf_op jit(solution)/shard_map/jit(_take)/gather | solution.py:94
  146.8 12.6 %multiply_reduce_fusion = (f32[96,24]{1,0:T(8,128)S(1)}, f32[96,24,256]{2,1,0:T(8,128)}) fusion(f32[96,256]{1,0:T(8,128)S(1)} %convert_element_type.29, bf16[96,256,256]{2,1,0:T(8,128)(2,1)} %param.15, bf16[96,24,256]{2,1,0:T(8,128)(2,1)S(1)} %copy-done.5, f32[]{:T(128)} %bitcast.24, f32[96,24,256]{2,1,0:T(8,128)} %param.13, ...), kind=kOutput, calls=%fused_computation.19 | convolution fusion | flops 309065472 | bytes 21055496 | tf_op jit(solution)/shard_map/fij,fhj->fhi/dot_general | solution.py:76
  159.5 19.3 %all_to_all.64 = f32[64,24,96]{2,1,0:T(8,128)S(1)} all-to-all(f32[64,24,96]{2,1,0:T(8,128)S(1)} %broadcast_in_dim.63), channel_id=1, replica_groups=mesh['grp'=4,'dev_0'=4,'dev_1'=4,'dev_2'=2] {'grp','dev_0','dev_1'}, dimensions={0} | all-to-all | bytes 1179648 | tf_op jit(solution)/shard_map/all_to_all | solution.py:26
  178.8 0.1 broadcast_in_dim.64
  178.9 6.5 %all_to_all.65 = f32[2,64,24,96]{3,2,1,0:T(8,128)S(1)} all-to-all(f32[2,64,24,96]{3,2,1,0:T(8,128)S(1)} %broadcast_in_dim.64), channel_id=1, replica_groups=mesh['grp'=4,'dev_0'=4,'dev_1'=4,'dev_2'=2] {'dev_2'}, dimensions={0} | all-to-all | bytes 2359296 | tf_op jit(solution)/shard_map/all_to_all | solution.py:26
  185.4 0.1 copy.44
  185.5 0.3 copy.45
  185.8 0.9 reshape.76
  186.8 3.8 %divide_convert_fusion = (bf16[24,128]{1,0:T(8,128)(2,1)S(1)}, f32[24,128]{1,0:T(8,128)S(1)}) fusion(f32[128]{0:T(128)S(1)} %get-tuple-element.3, f32[24,12288]{1,0:T(8,128)S(1)} %reshape.76, s32[128]{0:T(128)S(1)} %iota_add_fusion, s32[12288]{0:T(1024)S(1)} %bitcast.91, f32[24,128]{1,0:T(8,128)S(1)} %copy-done.6, f32[24,128]{1,0:T(8,128)S(1)} %copy-done.3, ...), kind=kOutput, calls=%fused_computation.48 | convolution fusion | flops 454585344 | bytes 1285128 | tf_op jit(solution)/shard_map/dot_general | solution.py:81
  190.6 15.2 %all_to_all.66 = bf16[64,24,128]{2,1,0:T(8,128)(2,1)S(1)} all-to-all(bf16[64,24,128]{2,1,0:T(8,128)(2,1)S(1)} %broadcast_in_dim.65), channel_id=1, replica_groups=mesh['grp'=4,'dev_0'=4,'dev_1'=4,'dev_2'=2] {'grp','dev_0','dev_1'}, dimensions={0} | all-to-all | bytes 786432 | tf_op jit(solution)/shard_map/all_to_all | solution.py:26
  205.8 0.1 broadcast_in_dim.66
  205.9 6.1 %all_to_all.67 = bf16[2,64,24,128]{3,2,1,0:T(8,128)(2,1)S(1)} all-to-all(bf16[2,64,24,128]{3,2,1,0:T(8,128)(2,1)S(1)} %broadcast_in_dim.66), channel_id=1, replica_groups=mesh['grp'=4,'dev_0'=4,'dev_1'=4,'dev_2'=2] {'dev_2'}, dimensions={0} | all-to-all | bytes 1572864 | tf_op jit(solution)/shard_map/all_to_all | solution.py:26
  212.1 2.9 %multiply_add_fusion.3 = (f32[24,128]{1,0:T(8,128)}, f32[24,128]{1,0:T(8,128)S(1)}) fusion(f32[]{:T(128)} %bitcast.23, f32[24,128]{1,0:T(8,128)S(1)} %copy-done.3, f32[24,128]{1,0:T(8,128)S(1)} %fusion.29, f32[]{:T(128)} %bitcast, f32[128]{0:T(128)S(1)} %get-tuple-element.3, f32[24,128]{1,0:T(8,128)S(1)} %get-tuple-element.18, ...), kind=kOutput, calls=%fused_computation.47 | convolution fusion | flops 100681728 | bytes 5042696 | tf_op jit(solution)/shard_map/hk,bk->hb/dot_general | solution.py:85
  215.1 19.5 %all_to_all.68 = f32[64,24,128]{2,1,0:T(8,128)S(1)} all-to-all(f32[64,24,128]{2,1,0:T(8,128)S(1)} %broadcast_in_dim.67), channel_id=1, replica_groups=mesh['grp'=4,'dev_0'=4,'dev_1'=4,'dev_2'=2] {'grp','dev_0','dev_1'}, dimensions={0} | all-to-all | bytes 1572864 | tf_op jit(solution)/shard_map/all_to_all | solution.py:26
  234.6 0.1 broadcast_in_dim.68
  234.7 6.5 %all_to_all.69 = f32[2,64,24,128]{3,2,1,0:T(8,128)S(1)} all-to-all(f32[2,64,24,128]{3,2,1,0:T(8,128)S(1)} %broadcast_in_dim.68), channel_id=1, replica_groups=mesh['grp'=4,'dev_0'=4,'dev_1'=4,'dev_2'=2] {'dev_2'}, dimensions={0} | all-to-all | bytes 3145728 | tf_op jit(solution)/shard_map/all_to_all | solution.py:26
  241.2 0.1 copy.48
  241.4 4.6 %copy.49 = f32[24,128,128]{0,2,1:T(8,128)} copy(f32[24,128,128]{2,0,1:T(8,128)S(1)} %bitcast.83) | data formatting | bytes 3145728 | tf_op jit(solution)/shard_map/transpose | solution.py:30
  246.0 4.0 %gather_fusion.1 = f32[96,24]{1,0:T(8,128)S(1)} fusion(f32[24,16384]{0,1:T(8,128)} %bitcast.76, s32[1024]{0:T(1024)S(1)} %pad_clamp_fusion), kind=kCustom, calls=%fused_computation.1.clone | custom fusion | bytes 18816 | tf_op jit(solution)/shard_map/jit(_take)/gather | solution.py:94
  250.1 5.6 %multiply_add_fusion = f32[96,24,256]{2,1,0:T(8,128)} fusion(f32[96,24,256]{2,1,0:T(8,128)} %get-tuple-element.16, f32[96,24]{1,0:T(8,128)S(1)} %broadcast_select_fusion, f32[]{:T(128)} %bitcast.23, f32[96,256]{1,0:T(8,128)S(1)} %bitcast.88, f32[96,24,256]{2,1,0:T(8,128)} %param.13, f32[96,24,256]{2,1,0:T(8,128)} %get-tuple-element.12, ...), kind=kLoop, calls=%fused_computation.18 | loop fusion | flops 4718592 | bytes 9553928 | tf_op jit(solution)/shard_map/add | solution.py:95
  (37 shorter events, 0.8 us)
Async XLA Ops:
  13.9 13.0 %copy-start.8 = (s32[96]{0:T(128)S(1)}, s32[96]{0:T(128)}, u32[]{:S(2)}) copy-start(s32[96]{0:T(128)} %param.17) | copy-start | bytes 1156
  13.9 13.0 %copy-start.2 = (bf16[96,256]{1,0:T(8,128)(2,1)S(1)}, bf16[96,256]{1,0:T(8,128)(2,1)}, u32[]{:S(2)}) copy-start(bf16[96,256]{1,0:T(8,128)(2,1)} %param.16) | copy-start | bytes 147460
  14.9 61.2 %all-to-all-start = ((f32[64,24,96]{2,1,0:T(8,128)}), f32[64,24,96]{2,1,0:T(8,128)S(1)}, u32[]{:S(2)}, u32[]{:S(2)}) async-start(f32[64,24,96]{2,1,0:T(8,128)} %broadcast_in_dim.57), calls=%async_computation | async-start | bytes 1572864 | tf_op jit(solution)/shard_map/all_to_all | solution.py:26
  26.9 45.3 %copy-start.7 = (f32[128]{0:T(128)S(1)}, f32[128]{0:T(128)}, u32[]{:S(2)}) copy-start(f32[128]{0:T(128)} %param.19) | copy-start | bytes 1540
  81.2 1.2 copy-start.3
  81.2 1.2 copy-start.6
  102.9 6.3 %copy-start = (bf16[128,16384]{1,0:T(8,128)(2,1)S(1)}, bf16[128,16384]{1,0:T(8,128)(2,1)}, u32[]{:S(2)}) copy-start(bf16[128,16384]{1,0:T(8,128)(2,1)} %param.18) | copy-start | bytes 12582916
  110.4 5.7 %copy-start.4 = (f32[2]{0:T(128)S(1)}, f32[2]{0:T(128)}, u32[]{:S(2)}) copy-start(f32[2]{0:T(128)} %param.23) | copy-start | bytes 28
  111.4 20.2 %all-to-all-start.4 = ((f32[64,24,128]{2,1,0:T(8,128)}), f32[64,24,128]{2,1,0:T(8,128)S(1)}, u32[]{:S(2)}, u32[]{:S(2)}) async-start(f32[64,24,128]{2,1,0:T(8,128)} %broadcast_in_dim.61), calls=%async_computation.4 | async-start | bytes 1572864 | tf_op jit(solution)/shard_map/all_to_all | solution.py:26
  138.0 8.7 %copy-start.5 = (bf16[96,24,256]{2,1,0:T(8,128)(2,1)S(1)}, bf16[96,24,256]{2,1,0:T(8,128)(2,1)}, u32[]{:S(2)}) copy-start(bf16[96,24,256]{2,1,0:T(8,128)(2,1)} %param.14) | copy-start | bytes 3538948
  205.8 6.3 %copy-start.1 = (bf16[128,16384]{1,0:T(8,128)(2,1)S(1)}, bf16[128,16384]{1,0:T(8,128)(2,1)}, u32[]{:S(2)}) copy-start(bf16[128,16384]{1,0:T(8,128)(2,1)} %param.18) | copy-start | bytes 12582916
where the time goes:
time: 257 us; the launch traced here: 256 us
  blocking collectives  144 us (56%)
  matrix products  46.7 us (18%)
  local copies, waits for them, and re-layouts  25.3 us (10%)
  starting transfers between devices  16.6 us (6%)
  waiting for transfers between devices  14.9 us (6%)
  other arithmetic  6.78 us (3%)
    all_to_all x10, blocking collectives, from_everyone(): return lax.all_to_all(copies, axis, split_axis=0, concat_axis=0, tiled=True)  107 us
    all_gather x1, blocking collectives, turned_gather(): filled = lax.all_gather(both, axis, axis=0, tiled=True)  36.9 us
    dot_general x2, matrix products, on_device(): jnp.einsum('fij,fhj->fhi', feeder_inverse, residual, preferred_element_ty...  23.7 us
    all_to_all x2, starting transfers between devices, from_everyone(): return lax.all_to_all(copies, axis, split_axis=0, concat_axis=0, tiled=True)  16.6 us
    all_to_all x2, waiting for transfers between devices, from_everyone(): return lax.all_to_all(copies, axis, split_axis=0, concat_axis=0, tiled=True)  14.9 us
    transpose x4, local copies, waits for them, and re-layouts, joined_along(): blocks = jnp.moveaxis(blocks, 0, dim)  9.86 us
    gather x2, local copies, waits for them, and re-layouts, on_device(): at_feeder = jnp.take(all_steps, feeder_bus, axis=1)  8 us
    dot_general x1, matrix products, on_device(): jnp.einsum('fij,fj->fi', feeder_inverse, coupling, preferred_element_type...  7.91 us
  transfers between devices with their start and end apart: 2, of which 1 were waited for; matrix products, arithmetic and copies ran while one was open for 5% of the time, Pallas kernels for 0%

commit v1 on v0

--- a/solution.py
+++ b/solution.py
@@ -11,7 +11,9 @@
     turned = [jnp.moveaxis(a, dim, 0) for a, dim in zip(arrays, dims)]
     widths = [t[0].size for t in turned]
     both = jnp.concatenate([t.reshape(-1, w) for t, w in zip(turned, widths)], axis=1)
-    filled = lax.all_gather(both, axis, axis=0, tiled=True)
+    filled = jnp.concatenate(
+        lax.all_to_all(jnp.stack([both] * lax.axis_size(axis)), axis, 0, 0), axis=0
+    )
     blocks = jnp.split(filled, [sum(widths[:k]) for k in range(1, len(widths))], axis=1)
     return tuple(
         (

time: 257 us -> 240 us (0.934)
  blocking collectives: 144 us -> 107 us
  waiting for transfers between devices: 14.9 us -> 25.9 us
  starting transfers between devices: 16.6 us -> 26.6 us
    all_gather x1 -> x0, blocking collectives: 36.9 us -> none  [turned_gather(): filled = lax.all_gather(both, axis, axis=0, tiled=True)]
    all_to_all x0 -> x1, starting transfers between devices: none -> 11.5 us  [turned_gather(): lax.all_to_all(jnp.stack([both] * lax.axis_size(axis)), axis, 0, 0)]
    all_to_all x2, waiting for transfers between devices: 14.9 us -> 25.9 us  [from_everyone(): return lax.all_to_all(copies, axis, split_axis=0, concat_axis=0, tiled=True)]
  transfers between devices with their start and end apart: 2 -> 3, of which waited for: 1 -> 2; matrix products, arithmetic and copies ran while one was open for 5% -> 7% of each run, Pallas kernels for 0% -> 0%
where the time goes in v1:
time: 240 us
  blocking collectives  107 us (45%)
  matrix products  46.5 us (19%)
  starting transfers between devices  26.6 us (11%)
  waiting for transfers between devices  25.9 us (11%)
  local copies, waits for them, and re-layouts  25.4 us (11%)
  other arithmetic  6.83 us (3%)
    all_to_all x10, blocking collectives, from_everyone(): return lax.all_to_all(copies, axis, split_axis=0, concat_axis=0, tiled=True)  107 us
    all_to_all x2, waiting for transfers between devices, from_everyone(): return lax.all_to_all(copies, axis, split_axis=0, concat_axis=0, tiled=True)  25.9 us
    dot_general x2, matrix products, on_device(): jnp.einsum('fij,fhj->fhi', feeder_inverse, residual, preferred_element_ty...  23.1 us
    all_to_all x2, starting transfers between devices, from_everyone(): return lax.all_to_all(copies, axis, split_axis=0, concat_axis=0, tiled=True)  15.2 us
    all_to_all x1, starting transfers between devices, turned_gather(): lax.all_to_all(jnp.stack([both] * lax.axis_size(axis)), axis, 0, 0)  11.5 us
    transpose x4, local copies, waits for them, and re-layouts, joined_along(): blocks = jnp.moveaxis(blocks, 0, dim)  9.89 us
    dot_general x1, matrix products, on_device(): jnp.einsum('fij,fj->fi', feeder_inverse, coupling, preferred_element_type...  8.06 us
    gather x2, local copies, waits for them, and re-layouts, on_device(): at_feeder = jnp.take(all_steps, feeder_bus, axis=1)  8 us
  transfers between devices with their start and end apart: 3, of which 2 were waited for; matrix products, arithmetic and copies ran while one was open for 7% of the time, Pallas kernels for 0%

profile of v1, /device:TPU:1, one launch (start us, length us, event | category | flops | bytes accessed | tf_op | source)
XLA Modules:
  0.0 239.6 jit_solution(10590095931794983814)
XLA Ops:
  0.6 0.7 compare_select_fusion
  1.4 8.1 %fusion.37 = f32[96,1,256]{2,1,0:T(1,128)S(1)} fusion(bf16[96,256,256]{2,1,0:T(8,128)(2,1)} %param.15, bf16[96,256,1]{1,0,2:T(8,128)(2,1)} %bitcast.84), kind=kOutput, calls=%fused_computation.40 | convolution fusion | flops 12582912 | bytes 12730368 | tf_op jit(solution)/shard_map/fij,fj->fi/dot_general | solution.py:59
  9.4 0.1 multiply_reduce_fusion.2
  9.6 0.7 stack.2
  10.3 11.5 %all-to-all-start.2 = ((f32[128,96,2]{1,2,0:T(2,128)}), f32[128,96,2]{1,2,0:T(2,128)S(1)}, u32[]{:S(2)}, u32[]{:S(2)}) async-start(f32[128,96,2]{1,2,0:T(2,128)} %stack.2), calls=%async_computation.2 | async-start | bytes 262144 | tf_op jit(solution)/shard_map/all_to_all | solution.py:15
  21.8 0.6 fusion.43
  22.5 10.4 %multiply_reduce_fusion.1 = (f32[96,24]{1,0:T(8,128)S(1)}, f32[96,24,256]{2,1,0:T(8,128)}) fusion(f32[96,256]{1,0:T(8,128)S(1)} %convert_element_type.29, bf16[96,256,256]{2,1,0:T(8,128)(2,1)} %param.15, bf16[96,24,256]{2,1,0:T(8,128)(2,1)} %param.14, f32[96,24,256]{2,1,0:T(8,128)S(1)} %copy-done.2, f32[]{:T(128)} %bitcast.1), kind=kOutput, calls=%fused_computation.21 | convolution fusion | flops 306706176 | bytes 18588676 | tf_op jit(solution)/shard_map/fij,fhj->fhi/dot_general | solution.py:78
  32.9 1.0 broadcast_in_dim.57
  33.9 10.5 %all-to-all-start = ((f32[64,24,96]{2,1,0:T(8,128)}), f32[64,24,96]{2,1,0:T(8,128)S(1)}, u32[]{:S(2)}, u32[]{:S(2)}) async-start(f32[64,24,96]{2,1,0:T(8,128)} %broadcast_in_dim.57), calls=%async_computation | async-start | bytes 1572864 | tf_op jit(solution)/shard_map/all_to_all | solution.py:28
  44.4 0.2 reshape.75
  44.7 3.9 %add_add_fusion = (f32[128]{0:T(128)S(1)}, f32[128]{0:T(128)S(1)}) fusion(f32[128]{0:T(128)S(1)} %copy-done.9, f32[]{:T(128)} %bitcast.23, f32[]{:T(128)} %bitcast.1, s32[128]{0:T(128)S(1)} %iota_add_fusion, s32[12288]{0:T(1024)S(1)} %bitcast.87, f32[12288,2]{0,1:T(2,128)S(1)} %reshape.75), kind=kOutput, calls=%fused_computation.55 | convolution fusion | flops 20447744 | bytes 100360 | tf_op jit(solution)/shard_map/dot_general | solution.py:70
  48.6 11.0 %all-to-all-done = f32[64,24,96]{2,1,0:T(8,128)S(1)} async-done(((f32[64,24,96]{2,1,0:T(8,128)}), f32[64,24,96]{2,1,0:T(8,128)S(1)}, u32[]{:S(2)}, u32[]{:S(2)}) %all-to-all-start) | async-done | bytes 589856 | tf_op jit(solution)/shard_map/all_to_all | solution.py:28
  59.7 0.1 broadcast_in_dim.58
  59.8 6.6 %all_to_all.65 = f32[2,64,24,96]{3,2,1,0:T(8,128)S(1)} all-to-all(f32[2,64,24,96]{3,2,1,0:T(8,128)S(1)} %broadcast_in_dim.58), channel_id=1, replica_groups=mesh['grp'=4,'dev_0'=4,'dev_1'=4,'dev_2'=2] {'dev_2'}, dimensions={0} | all-to-all | bytes 2359296 | tf_op jit(solution)/shard_map/all_to_all | solution.py:28
  66.3 0.1 copy.42
  66.5 0.3 copy.43
  66.8 0.9 reshape.72
  67.7 3.3 %divide_convert_fusion.1 = (bf16[24,128]{1,0:T(8,128)(2,1)S(1)}, f32[24,128]{1,0:T(8,128)S(1)}) fusion(f32[128]{0:T(128)S(1)} %get-tuple-element.4, f32[24,12288]{1,0:T(8,128)S(1)} %reshape.72, s32[128]{0:T(128)S(1)} %iota_add_fusion, s32[12288]{0:T(1024)S(1)} %bitcast.88, f32[24,128]{1,0:T(8,128)S(1)} %copy-done.8, f32[24,128]{1,0:T(8,128)S(1)} %copy-done.4, ...), kind=kOutput, calls=%fused_computation.50 | convolution fusion | flops 454579200 | bytes 1272836 | tf_op jit(solution)/shard_map/dot_general | solution.py:83
  71.1 15.2 %all_to_all.66 = bf16[64,24,128]{2,1,0:T(8,128)(2,1)S(1)} all-to-all(bf16[64,24,128]{2,1,0:T(8,128)(2,1)S(1)} %broadcast_in_dim.59), channel_id=1, replica_groups=mesh['grp'=4,'dev_0'=4,'dev_1'=4,'dev_2'=2] {'grp','dev_0','dev_1'}, dimensions={0} | all-to-all | bytes 786432 | tf_op jit(solution)/shard_map/all_to_all | solution.py:28
  86.3 0.1 broadcast_in_dim.60
  86.4 6.1 %all_to_all.67 = bf16[2,64,24,128]{3,2,1,0:T(8,128)(2,1)S(1)} all-to-all(bf16[2,64,24,128]{3,2,1,0:T(8,128)(2,1)S(1)} %broadcast_in_dim.60), channel_id=1, replica_groups=mesh['grp'=4,'dev_0'=4,'dev_1'=4,'dev_2'=2] {'dev_2'}, dimensions={0} | all-to-all | bytes 1572864 | tf_op jit(solution)/shard_map/all_to_all | solution.py:28
  92.6 1.2 fusion.29
  93.8 0.9 broadcast_in_dim.61
  94.8 4.6 %all-to-all-start.5 = ((f32[64,24,128]{2,1,0:T(8,128)}), f32[64,24,128]{2,1,0:T(8,128)S(1)}, u32[]{:S(2)}, u32[]{:S(2)}) async-start(f32[64,24,128]{2,1,0:T(8,128)} %broadcast_in_dim.61), calls=%async_computation.5 | async-start | bytes 1572864 | tf_op jit(solution)/shard_map/all_to_all | solution.py:28
  99.5 0.6 fusion.42
  100.1 14.9 %all-to-all-done.5 = f32[64,24,128]{2,1,0:T(8,128)S(1)} async-done(((f32[64,24,128]{2,1,0:T(8,128)}), f32[64,24,128]{2,1,0:T(8,128)S(1)}, u32[]{:S(2)}, u32[]{:S(2)}) %all-to-all-start.5) | async-done | bytes 786464 | tf_op jit(solution)/shard_map/all_to_all | solution.py:28
  115.1 6.2 %all_to_all.68 = f32[2,64,24,128]{3,2,1,0:T(8,128)S(1)} all-to-all(f32[2,64,24,128]{3,2,1,0:T(8,128)S(1)} %broadcast_in_dim.62), channel_id=1, replica_groups=mesh['grp'=4,'dev_0'=4,'dev_1'=4,'dev_2'=2] {'dev_2'}, dimensions={0} | all-to-all | bytes 3145728 | tf_op jit(solution)/shard_map/all_to_all | solution.py:28
  121.3 0.1 copy.47
  121.4 4.6 %copy.48 = f32[24,128,128]{0,2,1:T(8,128)} copy(f32[24,128,128]{2,0,1:T(8,128)S(1)} %bitcast.78) | data formatting | bytes 3145728 | tf_op jit(solution)/shard_map/transpose | solution.py:32
  126.1 4.0 %gather_fusion = f32[96,24]{1,0:T(8,128)S(1)} fusion(f32[24,16384]{0,1:T(8,128)} %bitcast.75, s32[1024]{0:T(1024)S(1)} %pad_clamp_fusion), kind=kCustom, calls=%fused_computation.clone | custom fusion | bytes 18816 | tf_op jit(solution)/shard_map/jit(_take)/gather | solution.py:96
  130.2 12.7 %multiply_reduce_fusion = (f32[96,24]{1,0:T(8,128)S(1)}, f32[96,24,256]{2,1,0:T(8,128)}) fusion(f32[96,256]{1,0:T(8,128)S(1)} %convert_element_type.29, bf16[96,256,256]{2,1,0:T(8,128)(2,1)} %param.15, bf16[96,24,256]{2,1,0:T(8,128)(2,1)S(1)} %copy-done.7, f32[]{:T(128)} %bitcast.23, f32[96,24,256]{2,1,0:T(8,128)} %param.13, ...), kind=kOutput, calls=%fused_computation.19 | convolution fusion | flops 309065472 | bytes 21055496 | tf_op jit(solution)/shard_map/fij,fhj->fhi/dot_general | solution.py:78
  143.0 19.3 %all_to_all.69 = f32[64,24,96]{2,1,0:T(8,128)S(1)} all-to-all(f32[64,24,96]{2,1,0:T(8,128)S(1)} %broadcast_in_dim.63), channel_id=1, replica_groups=mesh['grp'=4,'dev_0'=4,'dev_1'=4,'dev_2'=2] {'grp','dev_0','dev_1'}, dimensions={0} | all-to-all | bytes 1179648 | tf_op jit(solution)/shard_map/all_to_all | solution.py:28
  162.4 6.5 %all_to_all.70 = f32[2,64,24,96]{3,2,1,0:T(8,128)S(1)} all-to-all(f32[2,64,24,96]{3,2,1,0:T(8,128)S(1)} %broadcast_in_dim.64), channel_id=1, replica_groups=mesh['grp'=4,'dev_0'=4,'dev_1'=4,'dev_2'=2] {'dev_2'}, dimensions={0} | all-to-all | bytes 2359296 | tf_op jit(solution)/shard_map/all_to_all | solution.py:28
  168.9 0.1 copy.50
  169.0 0.3 copy.51
  169.4 0.9 reshape.82
  170.3 3.9 %divide_convert_fusion = (bf16[24,128]{1,0:T(8,128)(2,1)S(1)}, f32[24,128]{1,0:T(8,128)S(1)}) fusion(f32[128]{0:T(128)S(1)} %get-tuple-element.3, f32[24,12288]{1,0:T(8,128)S(1)} %reshape.82, s32[128]{0:T(128)S(1)} %iota_add_fusion, s32[12288]{0:T(1024)S(1)} %bitcast.89, f32[24,128]{1,0:T(8,128)S(1)} %copy-done.8, f32[24,128]{1,0:T(8,128)S(1)} %copy-done.4, ...), kind=kOutput, calls=%fused_computation.48 | convolution fusion | flops 454585344 | bytes 1285128 | tf_op jit(solution)/shard_map/dot_general | solution.py:83
  174.3 15.2 %all_to_all.71 = bf16[64,24,128]{2,1,0:T(8,128)(2,1)S(1)} all-to-all(bf16[64,24,128]{2,1,0:T(8,128)(2,1)S(1)} %broadcast_in_dim.65), channel_id=1, replica_groups=mesh['grp'=4,'dev_0'=4,'dev_1'=4,'dev_2'=2] {'grp','dev_0','dev_1'}, dimensions={0} | all-to-all | bytes 786432 | tf_op jit(solution)/shard_map/all_to_all | solution.py:28
  189.4 0.1 broadcast_in_dim.66
  189.5 6.1 %all_to_all.72 = bf16[2,64,24,128]{3,2,1,0:T(8,128)(2,1)S(1)} all-to-all(bf16[2,64,24,128]{3,2,1,0:T(8,128)(2,1)S(1)} %broadcast_in_dim.66), channel_id=1, replica_groups=mesh['grp'=4,'dev_0'=4,'dev_1'=4,'dev_2'=2] {'dev_2'}, dimensions={0} | all-to-all | bytes 1572864 | tf_op jit(solution)/shard_map/all_to_all | solution.py:28
  195.8 3.0 %multiply_add_fusion.3 = (f32[24,128]{1,0:T(8,128)}, f32[24,128]{1,0:T(8,128)S(1)}) fusion(f32[]{:T(128)} %bitcast.22, f32[24,128]{1,0:T(8,128)S(1)} %copy-done.4, f32[24,128]{1,0:T(8,128)S(1)} %fusion.29, f32[]{:T(128)} %bitcast, f32[128]{0:T(128)S(1)} %get-tuple-element.3, f32[24,128]{1,0:T(8,128)S(1)} %get-tuple-element.18, ...), kind=kOutput, calls=%fused_computation.47 | convolution fusion | flops 100681728 | bytes 5042696 | tf_op jit(solution)/shard_map/hk,bk->hb/dot_general | solution.py:87
  198.9 19.5 %all_to_all.73 = f32[64,24,128]{2,1,0:T(8,128)S(1)} all-to-all(f32[64,24,128]{2,1,0:T(8,128)S(1)} %broadcast_in_dim.67), channel_id=1, replica_groups=mesh['grp'=4,'dev_0'=4,'dev_1'=4,'dev_2'=2] {'grp','dev_0','dev_1'}, dimensions={0} | all-to-all | bytes 1572864 | tf_op jit(solution)/shard_map/all_to_all | solution.py:28
  218.4 0.1 broadcast_in_dim.68
  218.5 6.5 %all_to_all.74 = f32[2,64,24,128]{3,2,1,0:T(8,128)S(1)} all-to-all(f32[2,64,24,128]{3,2,1,0:T(8,128)S(1)} %broadcast_in_dim.68), channel_id=1, replica_groups=mesh['grp'=4,'dev_0'=4,'dev_1'=4,'dev_2'=2] {'dev_2'}, dimensions={0} | all-to-all | bytes 3145728 | tf_op jit(solution)/shard_map/all_to_all | solution.py:28
  225.0 0.1 copy.54
  225.1 4.6 %copy.55 = f32[24,128,128]{0,2,1:T(8,128)} copy(f32[24,128,128]{2,0,1:T(8,128)S(1)} %bitcast.81) | data formatting | bytes 3145728 | tf_op jit(solution)/shard_map/transpose | solution.py:32
  229.8 4.0 %gather_fusion.1 = f32[96,24]{1,0:T(8,128)S(1)} fusion(f32[24,16384]{0,1:T(8,128)} %bitcast.74, s32[1024]{0:T(1024)S(1)} %pad_clamp_fusion), kind=kCustom, calls=%fused_computation.1.clone | custom fusion | bytes 18816 | tf_op jit(solution)/shard_map/jit(_take)/gather | solution.py:96
  233.8 5.7 %multiply_add_fusion = f32[96,24,256]{2,1,0:T(8,128)} fusion(f32[96,24,256]{2,1,0:T(8,128)} %get-tuple-element.16, f32[96,24]{1,0:T(8,128)S(1)} %broadcast_select_fusion, f32[]{:T(128)} %bitcast.22, f32[96,256]{1,0:T(8,128)S(1)} %bitcast.86, f32[96,24,256]{2,1,0:T(8,128)} %param.13, f32[96,24,256]{2,1,0:T(8,128)} %get-tuple-element.12, ...), kind=kLoop, calls=%fused_computation.18 | loop fusion | flops 4718592 | bytes 9553928 | tf_op jit(solution)/shard_map/add | solution.py:97
  (43 shorter events, 1.0 us)
Async XLA Ops:
  1.4 8.1 %copy-start.3 = (bf16[96,256]{1,0:T(8,128)(2,1)S(1)}, bf16[96,256]{1,0:T(8,128)(2,1)}, u32[]{:S(2)}) copy-start(bf16[96,256]{1,0:T(8,128)(2,1)} %param.16) | copy-start | bytes 147460
  1.4 20.4 %copy-start.5 = (f32[2]{0:T(128)S(1)}, f32[2]{0:T(128)}, u32[]{:S(2)}) copy-start(f32[2]{0:T(128)} %param.22) | copy-start | bytes 28
  1.4 21.1 %copy-start.2 = (f32[96,24,256]{2,1,0:T(8,128)S(1)}, f32[96,24,256]{2,1,0:T(8,128)}, u32[]{:S(2)}) copy-start(f32[96,24,256]{2,1,0:T(8,128)} %param.13) | copy-start | bytes 7077892
  10.3 22.7 %all-to-all-start.2 = ((f32[128,96,2]{1,2,0:T(2,128)}), f32[128,96,2]{1,2,0:T(2,128)S(1)}, u32[]{:S(2)}, u32[]{:S(2)}) async-start(f32[128,96,2]{1,2,0:T(2,128)} %stack.2), calls=%async_computation.2 | async-start | bytes 262144 | tf_op jit(solution)/shard_map/all_to_all | solution.py:15
  32.9 11.8 %copy-start.9 = (f32[128]{0:T(128)S(1)}, f32[128]{0:T(128)}, u32[]{:S(2)}) copy-start(f32[128]{0:T(128)} %param.19) | copy-start | bytes 1540
  33.9 25.8 %all-to-all-start = ((f32[64,24,96]{2,1,0:T(8,128)}), f32[64,24,96]{2,1,0:T(8,128)S(1)}, u32[]{:S(2)}, u32[]{:S(2)}) async-start(f32[64,24,96]{2,1,0:T(8,128)} %broadcast_in_dim.57), calls=%async_computation | async-start | bytes 1572864 | tf_op jit(solution)/shard_map/all_to_all | solution.py:28
  66.5 1.2 copy-start.4
  66.5 1.2 copy-start.8
  86.3 6.3 %copy-start = (bf16[128,16384]{1,0:T(8,128)(2,1)S(1)}, bf16[128,16384]{1,0:T(8,128)(2,1)}, u32[]{:S(2)}) copy-start(bf16[128,16384]{1,0:T(8,128)(2,1)} %param.18) | copy-start | bytes 12582916
  93.8 5.7 %copy-start.6 = (f32[2]{0:T(128)S(1)}, f32[2]{0:T(128)}, u32[]{:S(2)}) copy-start(f32[2]{0:T(128)} %param.23) | copy-start | bytes 28
  93.8 6.3 %copy-start.10 = (s32[96]{0:T(128)S(1)}, s32[96]{0:T(128)}, u32[]{:S(2)}) copy-start(s32[96]{0:T(128)} %param.17) | copy-start | bytes 1156
  94.8 20.2 %all-to-all-start.5 = ((f32[64,24,128]{2,1,0:T(8,128)}), f32[64,24,128]{2,1,0:T(8,128)S(1)}, u32[]{:S(2)}, u32[]{:S(2)}) async-start(f32[64,24,128]{2,1,0:T(8,128)} %broadcast_in_dim.61), calls=%async_computation.5 | async-start | bytes 1572864 | tf_op jit(solution)/shard_map/all_to_all | solution.py:28
  121.4 8.7 %copy-start.7 = (bf16[96,24,256]{2,1,0:T(8,128)(2,1)S(1)}, bf16[96,24,256]{2,1,0:T(8,128)(2,1)}, u32[]{:S(2)}) copy-start(bf16[96,24,256]{2,1,0:T(8,128)(2,1)} %param.14) | copy-start | bytes 3538948
  189.4 6.3 %copy-start.1 = (bf16[128,16384]{1,0:T(8,128)(2,1)S(1)}, bf16[128,16384]{1,0:T(8,128)(2,1)}, u32[]{:S(2)}) copy-start(bf16[128,16384]{1,0:T(8,128)(2,1)} %param.18) | copy-start | bytes 12582916
